TPU v7x, 32 devices: a whole 2x2x4 slice. The times are simulated.
32 devices in a mesh: chan: 8 (over y, x, core), tm: 4 (over z).
Axes of the slice: x: 2, y: 2, z: 4, core: 2. Of those that a mesh axis runs over, the one named last changes fastest.
Arguments:
- voltages: bfloat16 [2, 8, 2048, 512], P(None, None, 'chan', 'tm'), may hold values from -0.25 to 0.25
- assignment: int32 [1024, 1], replicated, may hold values from 0 to 7; in each aligned block of 1024 rows (0 to 1023, 1024 to 2047, ...) at most 192 rows name the same one
- slot_subarray_index: int32 [8], replicated, may hold values from 0 to 7, each once
Outputs:
- visibilities: float32 [8, 8, 2, 384, 384], P('tm', 'chan')
Inputs may be any that keep to these rules, and one draw needn't show every extreme that they name: `assignment`: no subarray holds more than 192 antennas; one holds exactly 192. `slot_subarray_index`: each subarray appears once.
All inputs are finite; a program needn't handle non-finite values.
Results may differ from a plain program's by a relative error of at most 0.008.
Values may be sent and summed in bfloat16 or wider, within the bound.
No kernel may reach another device: no remote copies, remote signals or barrier semaphores. Data moves between devices by JAX's collectives and lax.ppermute only.
A program may use at most 64 MiB of HBM per device.

v0:
```python
import jax
import jax.numpy as jnp
from jax import lax
from jax.sharding import PartitionSpec as P

SLOT = 384


def result_slot_lookup(assignment, slot_subarray_index, subarrays, slots, inputs):
    owner = jnp.repeat(assignment[:, 0], 2)
    onehot = (owner[:, None] == jnp.arange(subarrays, dtype=jnp.int32)[None, :]).astype(jnp.int32)
    ranks = jnp.sum((jnp.cumsum(onehot, axis=0) - onehot) * onehot, axis=1)
    table = jnp.full((subarrays, slots), inputs, jnp.int32)
    table = table.at[owner, ranks].set(jnp.arange(inputs, dtype=jnp.int32))
    return table[slot_subarray_index].reshape(-1)


def compact(block, rows, subarrays, slots):
    parts, chans, inputs, samples = block.shape
    padded_voltages = jnp.concatenate(
        [block, jnp.zeros((parts, chans, 1, samples), block.dtype)], axis=2
    )
    picked = jnp.take(padded_voltages, rows, axis=2)
    picked = picked.reshape(parts, chans, subarrays, slots, samples)
    picked = jnp.transpose(picked, (2, 1, 0, 3, 4))
    return picked.reshape(subarrays, chans, 2 * slots, samples)


def gram(stacked):
    full = jnp.einsum("...pt,...qt->...pq", stacked, stacked, preferred_element_type=jnp.float32)
    half = stacked.shape[-2] // 2
    real = full[..., :half, :half] + full[..., half:, half:]
    imag = full[..., half:, :half] - full[..., :half, half:]
    return jnp.stack([real, imag], axis=-3)


def shards(voltages, assignment, slot_subarray_index):
    subarrays = slot_subarray_index.shape[0]
    slots = SLOT
    inputs = 2 * assignment.shape[0]
    rows = result_slot_lookup(assignment, slot_subarray_index, subarrays, slots, inputs)
    local_samples = voltages.shape[3]
    time_groups = lax.axis_size("tm")
    stacked = compact(
        lax.all_to_all(voltages, "chan", split_axis=1, concat_axis=2, tiled=True),
        rows,
        subarrays,
        slots,
    )
    received = lax.all_to_all(stacked, "tm", split_axis=0, concat_axis=3, tiled=True)
    total = None
    for block_index in range(time_groups):
        piece = received[..., block_index * local_samples : (block_index + 1) * local_samples]
        rounded = gram(piece).astype(jnp.bfloat16).astype(jnp.float32)
        total = rounded if total is None else total + rounded
    return total


def solution(mesh):
    placed = (P(None, None, "chan", "tm"), P(), P())
    return jax.shard_map(
        shards,
        mesh=mesh,
        in_specs=placed,
        out_specs=P("tm", "chan", None, None, None),
        check_vma=False,
    )
```

profile of v0, /device:TPU:0, one launch (start us, length us, event | category | flops | bytes accessed | tf_op | source)
XLA Modules:
  0.0 84.1 jit_solution(1011175587574448796)
XLA Ops:
  0.0 2.3 %copy.13 = bf16[2,8,256,128]{3,2,0,1:T(8,128)(2,1)} copy(bf16[2,8,256,128]{3,2,1,0:T(8,128)(2,1)} %param.3) | data formatting | bytes 2097152 | tf_op args[0]
  2.3 0.0 copy-start
  2.3 0.0 copy-start.3
  2.3 5.3 %all-to-all-start = ((bf16[2,8,256,128]{3,2,0,1:T(8,128)(2,1)}), bf16[2,8,256,128]{3,2,0,1:T(8,128)(2,1)S(1)}, u32[]{:S(2)}, u32[]{:S(2)}) async-start(bf16[2,8,256,128]{3,2,0,1:T(8,128)(2,1)} %copy.13), calls=%async_computation | async-start | bytes 2097152 | tf_op jit(solution)/shard_map/all_to_all | solution.py:45
  7.6 0.0 copy-start.2
  7.6 0.0 copy-start.1
  7.6 0.0 copy-done
  7.7 0.2 broadcast_in_dim.30
  7.9 0.3 eq.23
  8.1 0.3 reshape.321
  8.4 0.0 copy-done.3
  8.5 0.6 broadcast.137
  9.1 0.7 reduce.9
  9.8 0.1 broadcast_in_dim.31
  9.9 0.1 copy.11
  10.0 0.1 copy.12
  10.0 2.3 %reduce-window.6 = s32[8,16,128]{2,1,0:T(8,128)S(1)} reduce-window(s32[8,16,128]{2,1,0:T(8,128)S(1)} %fusion.19, s32[]{:T(128)} %constant.11.clone.1), window={size=1x1x128 pad=0_0x0_0x127_0}, to_apply=%region_0.0 | reduce-window | flops 2080768 | bytes 131076 | tf_op jit(solution)/shard_map/reduce-window
  12.3 0.3 slice_reduce_fusion
  12.6 0.2 reduce-window.9
  12.8 0.1 add_bitcast_fusion
  13.0 0.0 copy-done.2
  13.0 0.1 and_reduce_fusion
  13.1 0.0 copy-done.1
  13.1 0.1 multiply_reduce_fusion
  13.2 8.1 %scatter_custom_fusion = s32[3072]{0:T(1024)S(1)} fusion(s32[2048]{0:T(1024)S(1)} %broadcast_select_fusion, s32[2048]{0:T(1024)S(1)} %iota.11, s32[]{:T(128)} %constant.10.clone.1), kind=kCustom, calls=%fused_computation.57 | custom fusion | bytes 12292
  21.3 0.6 gather_fusion
  21.9 1.1 %all-to-all-done = bf16[2,8,256,128]{3,2,0,1:T(8,128)(2,1)S(1)} async-done(((bf16[2,8,256,128]{3,2,0,1:T(8,128)(2,1)}), bf16[2,8,256,128]{3,2,0,1:T(8,128)(2,1)S(1)}, u32[]{:S(2)}, u32[]{:S(2)}) %all-to-all-start) | async-done | bytes 1048608 | tf_op jit(solution)/shard_map/all_to_all | solution.py:45
  23.0 1.1 %copy.14 = bf16[2,8,256,128]{3,0,2,1:T(2,128)(2,1)S(1)} copy(bf16[2,8,256,128]{3,2,0,1:T(8,128)(2,1)S(1)} %all-to-all-done) | data formatting | bytes 2097152 | tf_op jit(solution)/shard_map/all_to_all | solution.py:45
  24.1 1.0 %pad_bitcast_fusion = bf16[2,2049,128]{2,0,1:T(2,128)(2,1)S(1)} fusion(bf16[2,1,2048,128]{3,0,2,1:T(2,128)(2,1)S(1)} %bitcast.90), kind=kLoop, calls=%fused_computation.26 | loop fusion | bytes 2097664 | tf_op jit(solution)/shard_map/concatenate | solution.py:20
  25.1 10.4 %gather_fusion.1 = bf16[3072,2,128]{2,1,0:T(2,128)(2,1)S(1)} fusion(bf16[2,2049,128]{2,0,1:T(2,128)(2,1)S(1)} %pad_bitcast_fusion, s32[3072]{0:T(1024)S(1)} %broadcast_clamp_fusion), kind=kCustom, calls=%fused_computation.1 | custom fusion | bytes 3158016 | tf_op jit(solution)/shard_map/jit(_take)/gather | solution.py:23
  35.5 0.8 copy_select_fusion
  36.3 41.2 %all_to_all.30 = bf16[8,1,768,128]{3,2,1,0:T(8,128)(2,1)S(1)} all-to-all(bf16[8,1,768,128]{3,2,1,0:T(8,128)(2,1)S(1)} %bitcast.88), channel_id=1, replica_groups=mesh['chan'=8,'tm'=4] {'tm'}, dimensions={0} | all-to-all | bytes 3145728 | tf_op jit(solution)/shard_map/all_to_all | solution.py:50
  77.5 0.3 copy.25
  77.8 0.8 convolution_bitcast_fusion
  78.6 0.8 convolution_bitcast_fusion.1
  79.3 0.8 convolution_bitcast_fusion.2
  80.1 0.8 convolution_bitcast_fusion.3
  80.9 0.3 fusion.14
  81.2 0.3 fusion.12
  81.4 0.3 fusion.10
  81.7 0.3 fusion.8
  82.0 0.5 convert_add_fusion
  82.5 1.6 %copy.18 = f32[2,1,2,384,384]{4,3,2,1,0:T(8,128)} copy(f32[2,1,2,384,384]{4,3,0,2,1:T(8,128)S(1)} %convert_add_fusion) | data formatting | bytes 4718592 | tf_op jit(solution)/shard_map/add | solution.py:55
  (13 shorter events, 0.2 us)
Async XLA Ops:
  2.3 5.4 %copy-start = (s32[1024,1]{0,1:T(1,128)S(1)}, s32[1024,1]{0,1:T(1,128)}, u32[]{:S(2)}) copy-start(s32[1024,1]{0,1:T(1,128)} %param.4) | copy-start | bytes 12292
  2.3 6.1 %copy-start.3 = (s32[8]{0:T(128)S(1)}, s32[8]{0:T(128)}, u32[]{:S(2)}) copy-start(s32[8]{0:T(128)} %param.5) | copy-start | bytes 100
  2.3 20.7 %all-to-all-start = ((bf16[2,8,256,128]{3,2,0,1:T(8,128)(2,1)}), bf16[2,8,256,128]{3,2,0,1:T(8,128)(2,1)S(1)}, u32[]{:S(2)}, u32[]{:S(2)}) async-start(bf16[2,8,256,128]{3,2,0,1:T(8,128)(2,1)} %copy.13), calls=%async_computation | async-start | bytes 2097152 | tf_op jit(solution)/shard_map/all_to_all | solution.py:45
  7.6 5.3 %copy-start.2 = (s32[2]{0:T(128)S(1)}, s32[2]{0:T(128)}, u32[]{:S(2)}) copy-start(s32[2]{0:T(128)} %constant.36) | copy-start | bytes 28
  7.6 5.4 %copy-start.1 = (s32[2]{0:T(128)S(1)}, s32[2]{0:T(128)}, u32[]{:S(2)}) copy-start(s32[2]{0:T(128)} %constant.33) | copy-start | bytes 28
where the time goes:
time: 84.3 us; the launch traced here: 84.1 us
  blocking collectives  41.2 us (49%)
  local copies, waits for them, and re-layouts  27.2 us (32%)
  other arithmetic  5.91 us (7%)
  starting transfers between devices  5.33 us (6%)
  matrix products  3.09 us (4%)
  waiting for transfers between devices  1.08 us (1%)
    all_to_all x1, blocking collectives, shards(): lax.all_to_all(stacked, 'tm', split_axis=0, concat_axis=3, tiled=True)  41.2 us
    unnamed x12, local copies, waits for them, and re-layouts  11 us
    gather x1, local copies, waits for them, and re-layouts, compact(): picked = jnp.take(padded_voltages, rows, axis=2)  10.4 us
    all_to_all x1, starting transfers between devices, shards(): lax.all_to_all(voltages, 'chan', split_axis=1, concat_axis=2, tiled=True)  5.33 us
    dot_general x4, matrix products, gram(): jnp.einsum('...pt,...qt->...pq', stacked, stacked, preferred_element_type...  3.09 us
    another operation x2, other arithmetic  2.45 us
  transfers between devices with their start and end apart: 1, of which 1 were waited for; matrix products, arithmetic and copies ran while one was open for 17% of the time, Pallas kernels for 0%

commit v1 on v0

--- a/solution.py
+++ b/solution.py
@@ -4,6 +4,12 @@
 from jax.sharding import PartitionSpec as P
 
 SLOT = 384
+
+
+def exchange_blocks(x, mesh_axis, split, join):
+    pieces = jnp.split(x, lax.axis_size(mesh_axis), axis=split)
+    incoming = lax.all_to_all(jnp.stack(pieces), mesh_axis, 0, 0)
+    return jnp.concatenate(incoming, axis=join)
 
 
 def result_slot_lookup(assignment, slot_subarray_index, subarrays, slots, inputs):
@@ -41,12 +47,7 @@
     rows = result_slot_lookup(assignment, slot_subarray_index, subarrays, slots, inputs)
     local_samples = voltages.shape[3]
     time_groups = lax.axis_size("tm")
-    stacked = compact(
-        lax.all_to_all(voltages, "chan", split_axis=1, concat_axis=2, tiled=True),
-        rows,
-        subarrays,
-        slots,
-    )
+    stacked = compact(exchange_blocks(voltages, "chan", 1, 2), rows, subarrays, slots)
     received = lax.all_to_all(stacked, "tm", split_axis=0, concat_axis=3, tiled=True)
     total = None
     for block_index in range(time_groups):

time: 84.3 us -> 102 us (1.21)
  local copies, waits for them, and re-layouts: 27.2 us -> 45.1 us
    unnamed x12 -> x18, local copies, waits for them, and re-layouts: 11 us -> 19.7 us
    reshape x0 -> x1, local copies, waits for them, and re-layouts: none -> 8.68 us  [exchange_blocks(): return jnp.concatenate(incoming, axis=join)]
    another operation x0 -> x1, local copies, waits for them, and re-layouts: none -> 1.57 us  [exchange_blocks(): incoming = lax.all_to_all(jnp.stack(pieces), mesh_axis, 0, 0)]
  transfers between devices with their start and end apart: 1 -> 1, of which waited for: 1 -> 1; matrix products, arithmetic and copies ran while one was open for 17% -> 14% of each run, Pallas kernels for 0% -> 0%
where the time goes in v1:
time: 102 us
  local copies, waits for them, and re-layouts  45.1 us (44%)
  blocking collectives  41.2 us (40%)
  other arithmetic  5.91 us (6%)
  starting transfers between devices  5.33 us (5%)
  matrix products  3.09 us (3%)
  waiting for transfers between devices  1.08 us (1%)
    all_to_all x1, blocking collectives, shards(): lax.all_to_all(stacked, 'tm', split_axis=0, concat_axis=3, tiled=True)  41.2 us
    unnamed x18, local copies, waits for them, and re-layouts  19.7 us
    gather x1, local copies, waits for them, and re-layouts, compact(): picked = jnp.take(padded_voltages, rows, axis=2)  10.4 us
    reshape x1, local copies, waits for them, and re-layouts, exchange_blocks(): return jnp.concatenate(incoming, axis=join)  8.68 us
    all_to_all x1, starting transfers between devices, exchange_blocks(): incoming = lax.all_to_all(jnp.stack(pieces), mesh_axis, 0, 0)  5.33 us
    dot_general x4, matrix products, gram(): jnp.einsum('...pt,...qt->...pq', stacked, stacked, preferred_element_type...  3.09 us
    another operation x2, other arithmetic  2.45 us
  transfers between devices with their start and end apart: 1, of which 1 were waited for; matrix products, arithmetic and copies ran while one was open for 14% of the time, Pallas kernels for 0%

profile of v1, /device:TPU:0, one launch (start us, length us, event | category | flops | bytes accessed | tf_op | source)
XLA Modules:
  0.0 102.0 jit_solution(3672793290934902290)
XLA Ops:
  0.0 1.6 %bitcast_dynamic-update-slice_fusion.7 = bf16[8,2,1,256,128]{4,3,1,2,0:T(8,128)(2,1)} fusion(bf16[2,8,256,128]{3,2,1,0:T(8,128)(2,1)} %param.3), kind=kLoop, calls=%fused_computation.46 | loop fusion | bytes 262144
  1.6 1.6 %bitcast_dynamic-update-slice_fusion.6 = bf16[8,2,1,256,128]{4,3,1,2,0:T(8,128)(2,1)} fusion(bf16[8,2,1,256,128]{4,3,1,2,0:T(8,128)(2,1)} %bitcast_dynamic-update-slice_fusion.7, bf16[2,8,256,128]{3,2,1,0:T(8,128)(2,1)} %param.3), kind=kLoop, calls=%fused_computation.45 | loop fusion | bytes 262144
  3.1 1.6 %bitcast_dynamic-update-slice_fusion.5 = bf16[8,2,1,256,128]{4,3,1,2,0:T(8,128)(2,1)} fusion(bf16[8,2,1,256,128]{4,3,1,2,0:T(8,128)(2,1)} %bitcast_dynamic-update-slice_fusion.6, bf16[2,8,256,128]{3,2,1,0:T(8,128)(2,1)} %param.3), kind=kLoop, calls=%fused_computation.44 | loop fusion | bytes 262144
  4.7 1.6 %bitcast_dynamic-update-slice_fusion.4 = bf16[8,2,1,256,128]{4,3,1,2,0:T(8,128)(2,1)} fusion(bf16[8,2,1,256,128]{4,3,1,2,0:T(8,128)(2,1)} %bitcast_dynamic-update-slice_fusion.5, bf16[2,8,256,128]{3,2,1,0:T(8,128)(2,1)} %param.3), kind=kLoop, calls=%fused_computation.43 | loop fusion | bytes 262144
  6.3 1.6 %bitcast_dynamic-update-slice_fusion.3 = bf16[8,2,1,256,128]{4,3,1,2,0:T(8,128)(2,1)} fusion(bf16[8,2,1,256,128]{4,3,1,2,0:T(8,128)(2,1)} %bitcast_dynamic-update-slice_fusion.4, bf16[2,8,256,128]{3,2,1,0:T(8,128)(2,1)} %param.3), kind=kLoop, calls=%fused_computation.42 | loop fusion | bytes 262144
  7.9 1.6 %bitcast_dynamic-update-slice_fusion.2 = bf16[8,2,1,256,128]{4,3,1,2,0:T(8,128)(2,1)} fusion(bf16[8,2,1,256,128]{4,3,1,2,0:T(8,128)(2,1)} %bitcast_dynamic-update-slice_fusion.3, bf16[2,8,256,128]{3,2,1,0:T(8,128)(2,1)} %param.3), kind=kLoop, calls=%fused_computation.41 | loop fusion | bytes 262144
  9.4 1.6 %bitcast_dynamic-update-slice_fusion.1 = bf16[8,2,1,256,128]{4,3,1,2,0:T(8,128)(2,1)} fusion(bf16[8,2,1,256,128]{4,3,1,2,0:T(8,128)(2,1)} %bitcast_dynamic-update-slice_fusion.2, bf16[2,8,256,128]{3,2,1,0:T(8,128)(2,1)} %param.3), kind=kLoop, calls=%fused_computation.40 | loop fusion | bytes 262144
  11.0 1.6 %bitcast_dynamic-update-slice_fusion = bf16[8,2,1,256,128]{4,3,1,2,0:T(8,128)(2,1)} fusion(bf16[8,2,1,256,128]{4,3,1,2,0:T(8,128)(2,1)} %bitcast_dynamic-update-slice_fusion.1, bf16[2,8,256,128]{3,2,1,0:T(8,128)(2,1)} %param.3), kind=kLoop, calls=%fused_computation.39 | loop fusion | bytes 262144 | tf_op jit(solution)/shard_map/stack | solution.py:11
  12.6 5.3 %all-to-all-start = ((bf16[8,2,1,256,128]{4,3,1,2,0:T(8,128)(2,1)}), bf16[8,2,1,256,128]{4,3,1,2,0:T(8,128)(2,1)S(1)}, u32[]{:S(2)}, u32[]{:S(2)}) async-start(bf16[8,2,1,256,128]{4,3,1,2,0:T(8,128)(2,1)} %bitcast_dynamic-update-slice_fusion), calls=%async_computation | async-start | bytes 2097152 | tf_op jit(solution)/shard_map/all_to_all | solution.py:11
  17.9 0.0 copy-start.1
  17.9 0.0 copy-done
  17.9 0.2 broadcast_in_dim.30
  18.1 0.3 eq.23
  18.4 0.3 reshape.324
  18.7 0.0 copy-done.3
  18.7 0.6 broadcast.137
  19.3 0.7 reduce.9
  20.0 0.1 broadcast_in_dim.31
  20.1 0.1 copy.26
  20.2 0.1 copy.27
  20.3 2.3 %reduce-window.6 = s32[8,16,128]{2,1,0:T(8,128)S(1)} reduce-window(s32[8,16,128]{2,1,0:T(8,128)S(1)} %fusion.19, s32[]{:T(128)} %constant.11.clone.1), window={size=1x1x128 pad=0_0x0_0x127_0}, to_apply=%region_0.0 | reduce-window | flops 2080768 | bytes 131076 | tf_op jit(solution)/shard_map/reduce-window
  22.6 0.3 slice_reduce_fusion
  22.9 0.2 reduce-window.9
  23.1 0.1 add_bitcast_fusion
  23.2 0.0 copy-done.2
  23.2 0.1 and_reduce_fusion
  23.3 0.0 copy-done.1
  23.3 0.1 multiply_reduce_fusion
  23.5 8.1 %scatter_custom_fusion = s32[3072]{0:T(1024)S(1)} fusion(s32[2048]{0:T(1024)S(1)} %broadcast_select_fusion, s32[2048]{0:T(1024)S(1)} %iota.11, s32[]{:T(128)} %constant.10.clone.1), kind=kCustom, calls=%fused_computation.65 | custom fusion | bytes 12292
  31.5 0.6 gather_fusion
  32.2 1.1 %all-to-all-done = bf16[8,2,1,256,128]{4,3,1,2,0:T(8,128)(2,1)S(1)} async-done(((bf16[8,2,1,256,128]{4,3,1,2,0:T(8,128)(2,1)}), bf16[8,2,1,256,128]{4,3,1,2,0:T(8,128)(2,1)S(1)}, u32[]{:S(2)}, u32[]{:S(2)}) %all-to-all-start) | async-done | bytes 1048608 | tf_op jit(solution)/shard_map/all_to_all | solution.py:11
  33.3 0.1 copy.36
  33.4 8.7 %copy.37 = bf16[2,1,2048,128]{3,0,2,1:T(2,128)(2,1)S(1)} copy(bf16[2,1,2048,128]{3,2,0,1:T(8,128)(2,1)S(1)} %bitcast.124) | data formatting | bytes 2097152 | tf_op jit(solution)/shard_map/reshape | solution.py:12
  42.1 1.0 pad_bitcast_fusion
  43.1 10.4 %gather_fusion.1 = bf16[3072,2,128]{2,1,0:T(2,128)(2,1)S(1)} fusion(bf16[2,2049,128]{2,0,1:T(2,128)(2,1)S(1)} %pad_bitcast_fusion, s32[3072]{0:T(1024)S(1)} %broadcast_clamp_fusion), kind=kCustom, calls=%fused_computation.1 | custom fusion | bytes 3158016 | tf_op jit(solution)/shard_map/jit(_take)/gather | solution.py:29
  53.5 0.8 copy_select_fusion
  54.3 41.2 %all_to_all.23 = bf16[8,1,768,128]{3,2,1,0:T(8,128)(2,1)S(1)} all-to-all(bf16[8,1,768,128]{3,2,1,0:T(8,128)(2,1)S(1)} %bitcast.122), channel_id=1, replica_groups=mesh['chan'=8,'tm'=4] {'tm'}, dimensions={0} | all-to-all | bytes 3145728 | tf_op jit(solution)/shard_map/all_to_all | solution.py:51
  95.5 0.3 copy.56
  95.8 0.8 convolution_bitcast_fusion
  96.5 0.8 convolution_bitcast_fusion.1
  97.3 0.8 convolution_bitcast_fusion.2
  98.1 0.8 convolution_bitcast_fusion.3
  98.9 0.3 fusion.14
  99.1 0.3 fusion.12
  99.4 0.3 fusion.10
  99.7 0.3 fusion.8
  99.9 0.5 convert_add_fusion
  100.5 1.6 %copy.41 = f32[2,1,2,384,384]{4,3,2,1,0:T(8,128)} copy(f32[2,1,2,384,384]{4,3,0,2,1:T(8,128)S(1)} %convert_add_fusion) | data formatting | bytes 4718592 | tf_op jit(solution)/shard_map/add | solution.py:56
  (16 shorter events, 0.2 us)
Async XLA Ops:
  6.3 11.6 %copy-start = (s32[1024,1]{0,1:T(1,128)S(1)}, s32[1024,1]{0,1:T(1,128)}, u32[]{:S(2)}) copy-start(s32[1024,1]{0,1:T(1,128)} %param.4) | copy-start | bytes 12292
  12.6 6.1 %copy-start.3 = (s32[8]{0:T(128)S(1)}, s32[8]{0:T(128)}, u32[]{:S(2)}) copy-start(s32[8]{0:T(128)} %param.5) | copy-start | bytes 100
  12.6 20.7 %all-to-all-start = ((bf16[8,2,1,256,128]{4,3,1,2,0:T(8,128)(2,1)}), bf16[8,2,1,256,128]{4,3,1,2,0:T(8,128)(2,1)S(1)}, u32[]{:S(2)}, u32[]{:S(2)}) async-start(bf16[8,2,1,256,128]{4,3,1,2,0:T(8,128)(2,1)} %bitcast_dynamic-update-slice_fusion), calls=%async_computation | async-start | bytes 2097152 | tf_op jit(solution)/shard_map/all_to_all | solution.py:11
  17.9 5.3 %copy-start.2 = (s32[2]{0:T(128)S(1)}, s32[2]{0:T(128)}, u32[]{:S(2)}) copy-start(s32[2]{0:T(128)} %constant.36) | copy-start | bytes 28
  17.9 5.4 %copy-start.1 = (s32[2]{0:T(128)S(1)}, s32[2]{0:T(128)}, u32[]{:S(2)}) copy-start(s32[2]{0:T(128)} %constant.33) | copy-start | bytes 28
